TPU v7x, 32 devices: a whole 2x2x4 slice. The times are simulated.
32 devices in a mesh: rep: 4 (over y, core), shard: 8 (over z, x).
Axes of the slice: x: 2, y: 2, z: 4, core: 2. Of those that a mesh axis runs over, the one named last changes fastest.
Arguments:
- hidden: bfloat16 [14336, 3584], P(('rep', 'shard')), may hold values from -144 to 144
- cotangent: bfloat16 [14336, 1024], P(('rep', 'shard')), may hold values from -6 to 6
- seq_ids: int32 [32, 448], P(('rep', 'shard')), may hold values from 0 to 3, as said below
- response_mask: int32 [32, 448], P(('rep', 'shard')), may hold values from 0 to 1, as said below
- group_ids: int32 [32, 4], P(('rep', 'shard')), may hold values from 0 to 15
- rewards: float32 [32, 4], P(('rep', 'shard')), may hold values from -6 to 6
- new_logp: float32 [32, 448], P(('rep', 'shard')), may hold values from -1.5 to -0.1
- old_logp: float32 [32, 448], P(('rep', 'shard')), may hold values from -1.5 to -0.1
- ref_logp: float32 [32, 448], P(('rep', 'shard')), may hold values from -1.5 to -0.1
- master: float32 [3, 3584, 1024], P(None, 'shard'), may hold values from -6 to 6
Outputs:
- new_master: float32 [3584, 1024], P('shard')
- rollout: bfloat16 [3, 3584, 2048], P(None, None, 'shard')
Inputs may be any that keep to these rules, and one draw needn't show every extreme that they name: `seq_ids`: each row numbers its device's 4 sequences in token order, never falling, each with one token or more. `response_mask`: within a sequence, prompt tokens come before response tokens; a sequence may have no response tokens.
All inputs are finite; a program needn't handle non-finite values.
Results may differ from a plain program's by a relative error of at most 0.0095.
Values may be sent and summed in bfloat16 or wider, within the bound.
A program may use at most 128 MiB of HBM per device.

v0:
```python
import jax
import jax.numpy as jnp
from jax import lax
from jax.sharding import PartitionSpec as P

HEAD = 128
KV_HEADS = 4
TP = 8
SEQ_DEV = 4


def token_coef(seq_row, mask_row, adv_row, new_row, old_row, ref_row):
    onehot = (seq_row[:, None] == jnp.arange(SEQ_DEV, dtype=jnp.int32)[None, :]).astype(jnp.float32)
    maskf = mask_row.astype(jnp.float32)
    lengths = jnp.maximum(jnp.dot(maskf, onehot, precision=lax.Precision.HIGHEST), 1.0)
    tok_len = jnp.dot(onehot, lengths, precision=lax.Precision.HIGHEST)
    tok_adv = jnp.dot(onehot, adv_row, precision=lax.Precision.HIGHEST)
    surrogate = -tok_adv * jnp.exp(new_row - old_row) + 0.2 * (1.0 - jnp.exp(ref_row - new_row))
    return maskf / tok_len * surrogate


def group_advantage(group_flat, reward_flat, stats):
    groups = stats.shape[1]
    onehot = (group_flat[:, None] == jnp.arange(groups, dtype=jnp.int32)[None, :]).astype(
        jnp.float32
    )
    count = jnp.maximum(stats[0], 1.0)
    mean = stats[1] / count
    spread = jnp.sqrt(jnp.maximum(stats[2] / count - mean * mean, 0.0))
    tok_mean = jnp.dot(onehot, mean, precision=lax.Precision.HIGHEST)
    tok_std = jnp.dot(onehot, jnp.maximum(spread, 0.5), precision=lax.Precision.HIGHEST)
    return (reward_flat - tok_mean) / tok_std


def group_sums(group_flat, reward_flat, groups):
    onehot = (group_flat[:, None] == jnp.arange(groups, dtype=jnp.int32)[None, :]).astype(
        jnp.float32
    )
    values = jnp.stack([jnp.ones_like(reward_flat), reward_flat, reward_flat * reward_flat], axis=0)
    return jnp.dot(values, onehot, precision=lax.Precision.HIGHEST)


def rounded(term):
    return lax.optimization_barrier(term.astype(jnp.bfloat16)).astype(jnp.float32)


def rollout_blocks(weights):
    layer_count = weights.shape[0]
    row_count = weights.shape[1]
    paired = weights.reshape(layer_count, row_count, 2, KV_HEADS, HEAD).transpose(0, 1, 3, 2, 4)
    paired = paired.reshape(layer_count, row_count, KV_HEADS, 2 * HEAD)
    by_rank = jnp.repeat(paired, TP // KV_HEADS, axis=2)
    copies = jnp.tile(by_rank, (1, 1, lax.axis_size("shard") // TP, 1))
    return copies.reshape(layer_count, row_count, lax.axis_size("shard") * 2 * HEAD)


def per_device(
    hidden,
    cotangent,
    seq_ids,
    response_mask,
    group_ids,
    rewards,
    new_logp,
    old_logp,
    ref_logp,
    master,
):
    n_rep = lax.axis_size("rep")
    n_shard = lax.axis_size("shard")
    groups = n_rep * n_shard * SEQ_DEV // 8
    rest_cols = lax.all_to_all(
        rollout_blocks(master[1:].astype(jnp.bfloat16)),
        "shard",
        split_axis=2,
        concat_axis=1,
        tiled=True,
    )
    local_sums = group_sums(group_ids[0], rewards[0], groups)
    stats = lax.psum(local_sums, ("rep", "shard"))
    advantage = group_advantage(group_ids[0], rewards[0], stats)
    coef = token_coef(
        seq_ids[0], response_mask[0], advantage, new_logp[0], old_logp[0], ref_logp[0]
    )
    delta = (coef[:, None] * cotangent.astype(jnp.float32)).astype(jnp.bfloat16)
    feature_count = hidden.shape[1]
    partial_value = lax.psum_scatter(
        rounded(
            lax.dot_general(
                hidden, delta, (((0,), (0,)), ((), ())), preferred_element_type=jnp.float32
            )
        ).astype(jnp.bfloat16),
        "shard",
        scatter_dimension=0,
        tiled=True,
    )
    grad = lax.psum(partial_value, "rep").astype(jnp.float32)
    squares = lax.psum(jnp.sum(grad * grad), "shard")
    rms = jnp.sqrt(squares / (feature_count * grad.shape[1]) + 1e-06)
    new_master = master[0] - 0.5 * grad / rms
    first_cols = lax.all_to_all(
        rollout_blocks(new_master[None].astype(jnp.bfloat16)),
        "shard",
        split_axis=2,
        concat_axis=1,
        tiled=True,
    )
    rollout = jnp.concatenate([first_cols, rest_cols], axis=0)
    return (new_master, rollout)


def solution(mesh):
    in_specs = (
        P(("rep", "shard"), None),
        P(("rep", "shard"), None),
        P(("rep", "shard"), None),
        P(("rep", "shard"), None),
        P(("rep", "shard"), None),
        P(("rep", "shard"), None),
        P(("rep", "shard"), None),
        P(("rep", "shard"), None),
        P(("rep", "shard"), None),
        P(None, "shard", None),
    )
    out_specs = (P("shard", None), P(None, None, "shard"))
    return jax.shard_map(
        per_device, mesh=mesh, in_specs=in_specs, out_specs=out_specs, check_vma=False
    )
```

profile of v0, /device:TPU:0, one launch (start us, length us, event | category | flops | bytes accessed | tf_op | source)
XLA Modules:
  0.0 468.4 jit_solution(8274017862780211825)
XLA Ops:
  9.0 41.9 %psum.21 = f32[3,16]{1,0:T(4,128)S(1)} all-reduce(f32[3,16]{1,0:T(4,128)S(1)} %fusion.15), channel_id=1, replica_groups=mesh['rep'=4,'shard'=8] {'rep','shard'}, use_global_device_ids=true, to_apply=%region_0.0 | all-reduce | flops 48 | bytes 384 | tf_op jit(solution)/shard_map/psum | solution.py:80
  55.3 1.0 fusion.11
  57.1 7.5 %fusion = bf16[3584,1024]{0,1:T(8,128)(2,1)} fusion(bf16[448,3584]{1,0:T(8,128)(2,1)S(1)} %copy-done, bf16[448,1024]{1,0:T(8,128)(2,1)} %param.11, f32[448]{0:T(512)S(1)} %add_multiply_fusion), kind=kOutput, calls=%fused_computation.1 | convolution fusion | flops 3293380608 | bytes 11470592 | tf_op jit(solution)/shard_map/dot_general | solution.py:89
  64.6 10.4 %copy.47 = bf16[3584,1024]{1,0:T(8,128)(2,1)} copy(bf16[3584,1024]{0,1:T(8,128)(2,1)} %fusion) | data formatting | bytes 14680064
  75.0 2.3 slice.36
  77.4 2.3 reshape.41
  79.6 5.7 %copy.49 = bf16[2,448,2,4,128]{1,0,4,2,3:T(2,128)(2,1)S(1)} copy(bf16[2,448,2,4,128]{4,3,2,1,0:T(4,128)(2,1)} %reshape.41) | data formatting | bytes 3670016 | tf_op jit(solution)/shard_map/transpose | solution.py:50
  85.3 4.2 broadcast_in_dim.15
  89.5 5.3 %all-to-all-start.1 = ((bf16[2,448,2048]{1,0,2:T(2,128)(2,1)}), bf16[2,448,2048]{1,0,2:T(2,128)(2,1)}, u32[]{:S(2)}, u32[]{:S(2)}) async-start(bf16[2,448,2048]{1,0,2:T(2,128)(2,1)} %bitcast.83), calls=%async_computation.1 | async-start | bytes 8388608 | tf_op jit(solution)/shard_map/all_to_all | solution.py:72
  94.9 188.3 %reduce-scatter.4.cloned.1.call-done = bf16[448,1024]{1,0:T(8,128)(2,1)} async-done(((bf16[3584,1024]{1,0:T(8,128)(2,1)}), bf16[448,1024]{1,0:T(8,128)(2,1)}) %reduce-scatter.4.cloned.1.call-update) | async-done | bytes 917520
  283.2 2.2 copy.48
  285.4 36.1 %all-reduce.2.cloned.1.call-done = bf16[448,1024]{0,1:T(8,128)(2,1)} async-done(((bf16[448,1024]{0,1:T(8,128)(2,1)}), bf16[448,1024]{0,1:T(8,128)(2,1)}) %all-reduce.2.cloned.1.call-update) | async-done | bytes 917520 | tf_op jit(solution)/shard_map/psum | solution.py:97
  321.5 2.4 fusion.3
  323.9 1.9 copy.51
  325.7 22.1 %psum.23 = f32[]{:T(128)} all-reduce(f32[]{:T(128)} %fusion.3), channel_id=1, replica_groups=mesh['rep'=4,'shard'=8] {'shard'}, use_global_device_ids=true, to_apply=%region_4.0 | all-reduce | flops 1 | bytes 8 | tf_op jit(solution)/shard_map/psum | solution.py:98
  348.6 3.0 fusion.36
  351.6 3.6 copy.33
  355.2 2.7 reshape.40
  358.6 2.5 broadcast_in_dim.6
  361.1 5.3 %broadcast_in_dim.14 = bf16[1,448,2048]{2,1,0:T(8,128)(2,1)} reshape(bf16[448,4,2,256]{3,2,1,0:T(2,128)(2,1)} %broadcast_in_dim.6) | data formatting | bytes 3670016 | tf_op jit(solution)/shard_map/broadcast_in_dim | solution.py:52
  366.4 10.7 %copy.35 = bf16[1,448,2048]{1,0,2:T(2,128)(2,1)} copy(bf16[1,448,2048]{2,1,0:T(8,128)(2,1)} %broadcast_in_dim.14) | data formatting | bytes 3670016 | tf_op jit(solution)/shard_map/broadcast_in_dim | solution.py:52
  377.6 15.4 %reduce = bf16[2048,448]{1,0:T(8,128)(2,1)} reduce(bf16[2048,1,448]{2,1,0:T(2,128)(2,1)} %bitcast.84, bf16[]{:T(256)} %broadcast.50), dimensions={1}, to_apply=%bitcast.77.reduce_sub_computation | reduce | bytes 3670018
  393.1 6.8 %reshape.57 = bf16[8,2,57344]{2,1,0:T(2,128)(2,1)} reshape(bf16[2048,448]{1,0:T(8,128)(2,1)} %reduce) | data formatting | bytes 3670016
  399.8 4.3 all-to-all-start
  404.2 11.1 %copy.46 = bf16[2,448,8,256]{3,1,2,0:T(8,128)(2,1)} copy(bf16[2,448,8,256]{1,0,3,2:T(2,128)(2,1)} %bitcast.27) | data formatting | bytes 7340032 | tf_op jit(solution)/shard_map/all_to_all | solution.py:72
  415.3 1.7 copy.42
  417.0 25.9 %all-to-all-done = bf16[8,2,57344]{2,1,0:T(2,128)(2,1)} async-done(((bf16[8,2,57344]{2,1,0:T(2,128)(2,1)}), bf16[8,2,57344]{2,1,0:T(2,128)(2,1)}, u32[]{:S(2)}, u32[]{:S(2)}) %all-to-all-start) | async-done | bytes 1835040 | tf_op jit(solution)/shard_map/all_to_all | solution.py:101
  442.9 7.2 %reshape.58 = bf16[2048,1,448]{2,1,0:T(2,128)(2,1)} reshape(bf16[8,2,57344]{2,1,0:T(2,128)(2,1)} %all-to-all-done) | data formatting | bytes 3670016
  450.1 2.8 copy.50
  452.9 3.0 copy.43
  455.8 2.0 copy.37
  458.4 2.9 pad_maximum_fusion
  (28 shorter events, 9.0 us)
Async XLA Ops:
  7.2 49.9 %copy-start = (bf16[448,3584]{1,0:T(8,128)(2,1)S(1)}, bf16[448,3584]{1,0:T(8,128)(2,1)}, u32[]{:S(2)}) copy-start(bf16[448,3584]{1,0:T(8,128)(2,1)} %param.10) | copy-start | bytes 9633796
  7.2 276.0 %reduce-scatter.4.cloned.1.call-start = ((), (), s32[]{:S(2)}) async-start(), calls=%async_computation.4 | async-start | bytes 8257536
  89.5 310.4 %all-to-all-start.1 = ((bf16[2,448,2048]{1,0,2:T(2,128)(2,1)}), bf16[2,448,2048]{1,0,2:T(2,128)(2,1)}, u32[]{:S(2)}, u32[]{:S(2)}) async-start(bf16[2,448,2048]{1,0,2:T(2,128)(2,1)} %bitcast.83), calls=%async_computation.1 | async-start | bytes 8388608 | tf_op jit(solution)/shard_map/all_to_all | solution.py:72
  94.8 226.7 %all-reduce.2.cloned.1.call-start = ((), (), s32[]{:S(2)}) async-start(), calls=%async_computation.3 | async-start | bytes 2097152 | tf_op jit(solution)/shard_map/psum | solution.py:97
  285.4 38.5 %slice-start = ((f32[3,448,1024]{2,1,0:T(8,128)}), f32[1,448,1024]{2,1,0:T(8,128)S(1)}, s32[]{:S(2)}) async-start(f32[3,448,1024]{2,1,0:T(8,128)} %param.19), calls=%async_computation.5 | async-start | bytes 3670016 | tf_op jit(solution)/shard_map/slice | solution.py:100
  323.9 24.7 %copy-start.3 = (bf16[448,1024]{0,1:T(8,128)(2,1)S(1)}, bf16[448,1024]{0,1:T(8,128)(2,1)}, u32[]{:S(2)}) copy-start(bf16[448,1024]{0,1:T(8,128)(2,1)} %all-reduce.2.cloned.1.call-done) | copy-start | bytes 2752516
  399.8 43.1 %all-to-all-start = ((bf16[8,2,57344]{2,1,0:T(2,128)(2,1)}), bf16[8,2,57344]{2,1,0:T(2,128)(2,1)}, u32[]{:S(2)}, u32[]{:S(2)}) async-start(bf16[8,2,57344]{2,1,0:T(2,128)(2,1)} %reshape.57), calls=%async_computation | async-start | bytes 3670016 | tf_op jit(solution)/shard_map/all_to_all | solution.py:101
  455.8 2.6 copy-start.2
  458.4 3.1 copy-start.1
Sparse Core Ops, SparseCore 0:
  75.2 207.9 reduce-scatter.3
  286.1 35.3 all-reduce.1
where the time goes:
time: 470 us; the launch traced here: 468 us
  waiting for transfers between devices  250 us (53%)
  local copies, waits for them, and re-layouts  90.3 us (19%)
  blocking collectives  64.1 us (14%)
  other arithmetic  26 us (6%)
  between operations  14.8 us (3%)
  matrix products  13.1 us (3%)
  starting transfers between devices  9.74 us (2%)
    unnamed x3, waiting for transfers between devices  188 us
    psum x1, blocking collectives, per_device(): stats = lax.psum(local_sums, ('rep', 'shard'))  41.9 us
    psum x1, waiting for transfers between devices, per_device(): grad = lax.psum(partial_value, 'rep').astype(jnp.float32)  36.1 us
    unnamed x16, local copies, waits for them, and re-layouts  34.2 us
    all_to_all x1, waiting for transfers between devices, per_device(): lax.all_to_all(rollout_blocks(new_master[None].astype(jnp.bfloat16)), 'sh...  25.9 us
    broadcast_in_dim x4, local copies, waits for them, and re-layouts, rollout_blocks(): by_rank = jnp.repeat(paired, TP // KV_HEADS, axis=2)  22.7 us
    psum x1, blocking collectives, per_device(): squares = lax.psum(jnp.sum(grad * grad), 'shard')  22.1 us
    unnamed x1, other arithmetic  15.4 us
  transfers between devices with their start and end apart: 4, of which 3 were waited for; matrix products, arithmetic and copies ran while one was open for 18% of the time, Pallas kernels for 0%

commit v1 on v0

--- a/solution.py
+++ b/solution.py
@@ -98,12 +98,12 @@
     squares = lax.psum(jnp.sum(grad * grad), "shard")
     rms = jnp.sqrt(squares / (feature_count * grad.shape[1]) + 1e-06)
     new_master = master[0] - 0.5 * grad / rms
-    first_cols = lax.all_to_all(
-        rollout_blocks(new_master[None].astype(jnp.bfloat16)),
-        "shard",
-        split_axis=2,
-        concat_axis=1,
-        tiled=True,
+    incoming_x = rollout_blocks(new_master[None].astype(jnp.bfloat16))
+    first_cols = jnp.concatenate(
+        lax.all_to_all(
+            jnp.stack(jnp.split(incoming_x, lax.axis_size("shard"), axis=2)), "shard", 0, 0
+        ),
+        axis=1,
     )
     rollout = jnp.concatenate([first_cols, rest_cols], axis=0)
     return (new_master, rollout)

time: 470 us -> 437 us (0.930)
  local copies, waits for them, and re-layouts: 90.3 us -> 69.7 us
  other arithmetic: 26 us -> 13.4 us
    unnamed x1 -> x0, other arithmetic: 15.4 us -> none
    broadcast_in_dim x4 -> x3, local copies, waits for them, and re-layouts: 22.7 us -> 11.9 us  [rollout_blocks(): by_rank = jnp.repeat(paired, TP // KV_HEADS, axis=2)]
    unnamed x16 -> x17, local copies, waits for them, and re-layouts: 34.2 us -> 27.8 us
    all_to_all x2 -> x0, local copies, waits for them, and re-layouts: 5 us -> none  [per_device(): lax.all_to_all(rollout_blocks(new_master[None].astype(jnp.bfloat16)), 'sh...]
  transfers between devices with their start and end apart: 4 -> 4, of which waited for: 3 -> 3; matrix products, arithmetic and copies ran while one was open for 18% -> 15% of each run, Pallas kernels for 0% -> 0%
where the time goes in v1:
time: 437 us; the launch traced here: 435 us
  waiting for transfers between devices  250 us (57%)
  local copies, waits for them, and re-layouts  69.7 us (16%)
  blocking collectives  64.1 us (15%)
  between operations  14.8 us (3%)
  other arithmetic  13.4 us (3%)
  matrix products  13.2 us (3%)
  starting transfers between devices  9.74 us (2%)
    unnamed x3, waiting for transfers between devices  188 us
    psum x1, blocking collectives, per_device(): stats = lax.psum(local_sums, ('rep', 'shard'))  41.9 us
    psum x1, waiting for transfers between devices, per_device(): grad = lax.psum(partial_value, 'rep').astype(jnp.float32)  36.1 us
    unnamed x17, local copies, waits for them, and re-layouts  27.8 us
    all_to_all x1, waiting for transfers between devices, per_device(): lax.all_to_all(jnp.stack(jnp.split(incoming_x, lax.axis_size('shard'), ax...  25.9 us
    psum x1, blocking collectives, per_device(): squares = lax.psum(jnp.sum(grad * grad), 'shard')  22.1 us
    broadcast_in_dim x3, local copies, waits for them, and re-layouts, rollout_blocks(): by_rank = jnp.repeat(paired, TP // KV_HEADS, axis=2)  11.9 us
    all_to_all x1, local copies, waits for them, and re-layouts, per_device(): lax.all_to_all(rollout_blocks(master[1:].astype(jnp.bfloat16)), 'shard',...  11.1 us
  transfers between devices with their start and end apart: 4, of which 3 were waited for; matrix products, arithmetic and copies ran while one was open for 15% of the time, Pallas kernels for 0%

profile of v1, /device:TPU:0, one launch (start us, length us, event | category | flops | bytes accessed | tf_op | source)
XLA Modules:
  0.0 435.2 jit_solution(58260634448328335)
XLA Ops:
  9.0 41.9 %psum.21 = f32[3,16]{1,0:T(4,128)S(1)} all-reduce(f32[3,16]{1,0:T(4,128)S(1)} %fusion.23), channel_id=1, replica_groups=mesh['rep'=4,'shard'=8] {'rep','shard'}, use_global_device_ids=true, to_apply=%region_0.0 | all-reduce | flops 48 | bytes 384 | tf_op jit(solution)/shard_map/psum | solution.py:80
  57.1 7.6 %fusion = bf16[3584,1024]{0,1:T(8,128)(2,1)} fusion(bf16[448,3584]{1,0:T(8,128)(2,1)S(1)} %copy-done, bf16[448,1024]{1,0:T(8,128)(2,1)} %param.11, f32[448]{0:T(512)S(1)} %add_multiply_fusion), kind=kOutput, calls=%fused_computation.1 | convolution fusion | flops 3293380608 | bytes 11470592 | tf_op jit(solution)/shard_map/dot_general | solution.py:89
  64.7 10.4 %copy.61 = bf16[3584,1024]{1,0:T(8,128)(2,1)} copy(bf16[3584,1024]{0,1:T(8,128)(2,1)} %fusion) | data formatting | bytes 14680064
  75.1 2.3 slice.36
  77.4 2.3 reshape.45
  79.7 5.7 %copy.63 = bf16[2,448,2,4,128]{1,0,4,2,3:T(2,128)(2,1)S(1)} copy(bf16[2,448,2,4,128]{4,3,2,1,0:T(4,128)(2,1)} %reshape.45) | data formatting | bytes 3670016 | tf_op jit(solution)/shard_map/transpose | solution.py:50
  85.4 4.2 broadcast_in_dim.15
  89.5 5.4 %all-to-all-start.1 = ((bf16[2,448,2048]{1,0,2:T(2,128)(2,1)}), bf16[2,448,2048]{1,0,2:T(2,128)(2,1)}, u32[]{:S(2)}, u32[]{:S(2)}) async-start(bf16[2,448,2048]{1,0,2:T(2,128)(2,1)} %bitcast.111), calls=%async_computation.1 | async-start | bytes 8388608 | tf_op jit(solution)/shard_map/all_to_all | solution.py:72
  94.9 188.3 %reduce-scatter.4.cloned.1.call-done = bf16[448,1024]{1,0:T(8,128)(2,1)} async-done(((bf16[3584,1024]{1,0:T(8,128)(2,1)}), bf16[448,1024]{1,0:T(8,128)(2,1)}) %reduce-scatter.4.cloned.1.call-update) | async-done | bytes 917520
  283.2 2.2 copy.62
  285.5 36.1 %all-reduce.2.cloned.1.call-done = bf16[448,1024]{0,1:T(8,128)(2,1)} async-done(((bf16[448,1024]{0,1:T(8,128)(2,1)}), bf16[448,1024]{0,1:T(8,128)(2,1)}) %all-reduce.2.cloned.1.call-update) | async-done | bytes 917520 | tf_op jit(solution)/shard_map/psum | solution.py:97
  321.6 2.4 fusion.3
  324.0 1.8 copy.64
  325.8 22.1 %psum.23 = f32[]{:T(128)} all-reduce(f32[]{:T(128)} %fusion.3), channel_id=1, replica_groups=mesh['rep'=4,'shard'=8] {'shard'}, use_global_device_ids=true, to_apply=%region_4.0 | all-reduce | flops 1 | bytes 8 | tf_op jit(solution)/shard_map/psum | solution.py:98
  348.7 3.0 fusion.44
  351.7 3.6 copy.51
  355.3 2.7 reshape.43
  358.7 2.5 broadcast_in_dim.6
  361.2 5.3 %broadcast_in_dim.14 = bf16[1,448,2048]{2,1,0:T(8,128)(2,1)} reshape(bf16[448,4,2,256]{3,2,1,0:T(2,128)(2,1)} %broadcast_in_dim.6) | data formatting | bytes 3670016 | tf_op jit(solution)/shard_map/broadcast_in_dim | solution.py:52
  366.4 1.7 fusion.17
  368.1 1.7 fusion.16
  369.8 1.6 fusion.15
  371.4 1.6 fusion.14
  373.1 1.6 fusion.13
  374.7 1.7 fusion.12
  376.4 1.7 fusion.11
  378.0 1.6 fusion.10
  379.7 4.3 all-to-all-start
  384.0 11.1 %copy.60 = bf16[2,448,8,256]{3,1,2,0:T(8,128)(2,1)} copy(bf16[2,448,8,256]{1,0,3,2:T(2,128)(2,1)} %bitcast.34) | data formatting | bytes 7340032 | tf_op jit(solution)/shard_map/all_to_all | solution.py:72
  395.1 1.7 copy.57
  396.8 25.9 %all-to-all-done = bf16[8,1,448,256]{3,2,1,0:T(8,128)(2,1)} async-done(((bf16[8,1,448,256]{3,2,1,0:T(8,128)(2,1)}), bf16[8,1,448,256]{3,2,1,0:T(8,128)(2,1)}, u32[]{:S(2)}, u32[]{:S(2)}) %all-to-all-start) | async-done | bytes 1835040 | tf_op jit(solution)/shard_map/all_to_all | solution.py:103
  422.7 5.7 %pad_maximum_fusion = bf16[3,3584,256]{2,1,0:T(8,128)(2,1)} fusion(bf16[2,3584,256]{2,1,0:T(8,128)(2,1)} %bitcast.112, bf16[1,3584,256]{2,1,0:T(8,128)(2,1)} %bitcast.30), kind=kLoop, calls=%fused_computation.2 | loop fusion | flops 2752512 | bytes 11010048 | tf_op jit(solution)/shard_map/concatenate | solution.py:108
  (26 shorter events, 8.8 us)
Async XLA Ops:
  7.2 49.9 %copy-start = (bf16[448,3584]{1,0:T(8,128)(2,1)S(1)}, bf16[448,3584]{1,0:T(8,128)(2,1)}, u32[]{:S(2)}) copy-start(bf16[448,3584]{1,0:T(8,128)(2,1)} %param.10) | copy-start | bytes 9633796
  7.2 276.1 %reduce-scatter.4.cloned.1.call-start = ((), (), s32[]{:S(2)}) async-start(), calls=%async_computation.4 | async-start | bytes 8257536
  89.5 290.1 %all-to-all-start.1 = ((bf16[2,448,2048]{1,0,2:T(2,128)(2,1)}), bf16[2,448,2048]{1,0,2:T(2,128)(2,1)}, u32[]{:S(2)}, u32[]{:S(2)}) async-start(bf16[2,448,2048]{1,0,2:T(2,128)(2,1)} %bitcast.111), calls=%async_computation.1 | async-start | bytes 8388608 | tf_op jit(solution)/shard_map/all_to_all | solution.py:72
  94.9 226.7 %all-reduce.2.cloned.1.call-start = ((), (), s32[]{:S(2)}) async-start(), calls=%async_computation.3 | async-start | bytes 2097152 | tf_op jit(solution)/shard_map/psum | solution.py:97
  285.5 38.5 %slice-start = ((f32[3,448,1024]{2,1,0:T(8,128)}), f32[1,448,1024]{2,1,0:T(8,128)S(1)}, s32[]{:S(2)}) async-start(f32[3,448,1024]{2,1,0:T(8,128)} %param.19), calls=%async_computation.5 | async-start | bytes 3670016 | tf_op jit(solution)/shard_map/slice | solution.py:100
  324.0 24.7 %copy-start.2 = (bf16[448,1024]{0,1:T(8,128)(2,1)S(1)}, bf16[448,1024]{0,1:T(8,128)(2,1)}, u32[]{:S(2)}) copy-start(bf16[448,1024]{0,1:T(8,128)(2,1)} %all-reduce.2.cloned.1.call-done) | copy-start | bytes 2752516
  379.7 43.1 %all-to-all-start = ((bf16[8,1,448,256]{3,2,1,0:T(8,128)(2,1)}), bf16[8,1,448,256]{3,2,1,0:T(8,128)(2,1)}, u32[]{:S(2)}, u32[]{:S(2)}) async-start(bf16[8,1,448,256]{3,2,1,0:T(8,128)(2,1)} %fusion.10), calls=%async_computation | async-start | bytes 3670016 | tf_op jit(solution)/shard_map/all_to_all | solution.py:103
  422.7 5.7 %copy-start.1 = (bf16[448,3584]{1,0:T(8,128)(2,1)S(1)}, bf16[448,3584]{1,0:T(8,128)(2,1)}, u32[]{:S(2)}) copy-start(bf16[448,3584]{1,0:T(8,128)(2,1)} %param.10) | copy-start | bytes 9633796
Sparse Core Ops, SparseCore 0:
  75.2 207.9 reduce-scatter.3
  286.2 35.3 all-reduce.1
